TPU v7x, 32 devices: a whole 2x2x4 slice. The times are simulated.
32 devices in a mesh: dp: 16 (over z, y, core), tensor: 2 (over x).
Axes of the slice: x: 2, y: 2, z: 4, core: 2. Of those that a mesh axis runs over, the one named last changes fastest.
Arguments:
- step: int32 [1], replicated, may hold values from 0 to 999
- activations: bfloat16 [2, 16384, 8192], P(None, 'dp', 'tensor'), may hold values from -6 to 6
- grad_weight: bfloat16 [2, 8192, 28672], P(None, 'tensor', 'dp'), may hold values from -6 to 6
Outputs:
- preconditioned: float32 [8192, 28672], P('tensor', 'dp')
All inputs are finite; a program needn't handle non-finite values.
Results may differ from a plain program's by a relative error of at most 0.0044.
Values may be sent and summed in bfloat16 or wider, within the bound.
No kernel may reach another device: no remote copies, remote signals or barrier semaphores. Data moves between devices by JAX's collectives and lax.ppermute only.
A program may use at most 192 MiB of HBM per device.

v0:
```python
import jax
import jax.numpy as jnp
from jax import lax
from jax.sharding import PartitionSpec as P

BLOCK = 1024
LAYERS = 2
ITERS = 4


def local(step, activations, grad_weight):
    groups = lax.axis_size("dp")
    layer = step[0] % LAYERS
    damping = 0.05 + 0.1 * step[0].astype(jnp.float32) / 1000.0
    acts = lax.dynamic_index_in_dim(activations, layer, 0, keepdims=False)
    grads = lax.dynamic_index_in_dim(grad_weight, layer, 0, keepdims=False)
    tok_rows = acts.shape[0]
    width = acts.shape[1]
    nblock = width // BLOCK
    share = BLOCK // groups
    blocks = acts.reshape(tok_rows, nblock, BLOCK)
    total_tokens = tok_rows * groups
    first = lax.axis_index("dp") * share
    summed = lax.psum(
        jnp.einsum("tkr,tkc->rkc", blocks, blocks, preferred_element_type=jnp.float32), "dp"
    )
    gram_rows = lax.dynamic_slice_in_dim(summed, first, share, 0)
    row_ids = first + lax.broadcasted_iota(jnp.int32, (share, 1, BLOCK), 0)
    col_ids = lax.broadcasted_iota(jnp.int32, (share, 1, BLOCK), 2)
    identity = (row_ids == col_ids).astype(jnp.float32)
    factor = gram_rows / total_tokens + damping * identity
    block_squares = lax.psum(jnp.sum(factor * factor, axis=(0, 2)), "dp")
    largest = lax.pmax(jnp.max(block_squares), "tensor")
    iterate = jnp.broadcast_to(identity / jnp.sqrt(largest), factor.shape)
    for sweep in range(ITERS):
        whole = lax.all_gather(iterate, "dp", axis=0, tiled=True)
        product = jnp.einsum("rkj,jkc->rkc", factor, whole, precision=lax.Precision.HIGHEST)
        iterate = 2.0 * iterate - jnp.einsum(
            "rkj,jkc->rkc", product, whole, precision=lax.Precision.HIGHEST
        )
    inverse = iterate.astype(jnp.bfloat16)
    stacked = grads.reshape(nblock, BLOCK, grads.shape[1])
    result = jnp.einsum(
        "rkc,kcf->krf",
        lax.all_gather(inverse, "dp", axis=0, tiled=True),
        stacked,
        preferred_element_type=jnp.float32,
    )
    return result.reshape(width, grads.shape[1])


def solution(mesh):
    in_specs = (P(), P(None, "dp", "tensor"), P(None, "tensor", "dp"))
    out_specs = P("tensor", "dp")
    return jax.shard_map(local, mesh=mesh, in_specs=in_specs, out_specs=out_specs, check_vma=False)
```

profile of v0, /device:TPU:0, one launch (start us, length us, event | category | flops | bytes accessed | tf_op | source)
XLA Modules:
  0.0 1019.5 jit_solution(3891566731821359104)
XLA Ops:
  6.5 0.0 all-reduce.2.cloned.1.call-start
  7.2 7.9 constant_dynamic-slice_fusion.1
  15.1 12.0 %copy.23 = bf16[1,1024,4096]{1,2,0:T(8,128)(2,1)} copy(bf16[1,1024,4096]{2,1,0:T(8,128)(2,1)} %constant_dynamic-slice_fusion.1) | data formatting | bytes 16777216
  27.1 17.1 %convolution_bitcast_fusion = f32[1024,4,1024]{2,0,1:T(8,128)} fusion(bf16[1024,4,1024]{0,2,1:T(8,128)(2,1)} %bitcast.51), kind=kOutput, calls=%fused_computation | convolution fusion | flops 8589934592 | bytes 25165824 | tf_op jit(solution)/shard_map/tkr,tkc->rkc/dot_general | solution.py:25
  44.2 0.0 all-reduce.2.cloned.1.call-update
  44.3 0.0 all-gather.14.cloned.1.call-start
  44.3 0.1 fusion.18
  44.4 300.7 %all-reduce.2.cloned.1.call-done = f32[1024,4,1024]{2,0,1:T(8,128)} async-done(((f32[1024,4,1024]{2,0,1:T(8,128)}), f32[1024,4,1024]{2,0,1:T(8,128)}) %all-reduce.2.cloned.1.call-update) | async-done | bytes 16777232 | tf_op jit(solution)/shard_map/psum | solution.py:24
  345.1 1.5 multiply_reduce_fusion
  346.6 31.8 %psum.15 = f32[4]{0:T(128)S(1)} all-reduce(f32[4]{0:T(128)S(1)} %multiply_reduce_fusion), channel_id=1, replica_groups=mesh['dp'=16,'tensor'=2] {'dp'}, use_global_device_ids=true, to_apply=%region_2.3 | all-reduce | flops 4 | bytes 32 | tf_op jit(solution)/shard_map/psum | solution.py:32
  378.4 0.6 reduce_max.9
  379.0 5.5 pmax.7
  385.2 0.8 broadcast_multiply_fusion
  386.0 0.0 all-gather.14.cloned.1.call-update
  386.0 0.3 all-gather.6.cloned.1.call-start
  386.3 47.5 %all-gather.14.cloned.1.call-done = f32[1024,1024]{1,0:T(8,128)} async-done(((f32[64,1024]{1,0:T(8,128)}), f32[1024,1024]{1,0:T(8,128)}) %all-gather.14.cloned.1.call-update) | async-done | bytes 4194320 | tf_op jit(solution)/shard_map/all_gather | solution.py:36
  433.8 11.8 %fusion.4 = f32[64,4,1024]{2,0,1:T(8,128)S(1)} fusion(f32[1024,1024]{1,0:T(8,128)} %all-gather.14.cloned.1.call-done, f32[1024,4,1024]{2,0,1:T(8,128)} %all-reduce.2.cloned.1.call-done, s32[]{:T(128)S(6)} %select_n.18, f32[64,1024]{1,0:T(8,128)S(1)} %fusion.18), kind=kOutput, calls=%fused_computation.5 | convolution fusion | flops 3221749760 | bytes 6553604 | tf_op jit(solution)/shard_map/rkj,jkc->rkc/dot_general | solution.py:37
  445.6 12.8 %fusion.10 = f32[64,4,1024]{2,0,1:T(8,128)} fusion(f32[64,4,1024]{2,0,1:T(8,128)S(1)} %fusion.4, f32[1024,1024]{1,0:T(8,128)} %all-gather.14.cloned.1.call-done, f32[64,1024]{1,0:T(8,128)S(1)} %get-tuple-element.5), kind=kOutput, calls=%fused_computation.7 | convolution fusion | flops 3221487616 | bytes 6553600 | tf_op jit(solution)/shard_map/rkj,jkc->rkc/dot_general | solution.py:38
  458.3 0.0 copy-start.4
  458.3 0.0 all-gather.6.cloned.1.call-update
  458.4 0.0 all-gather.8.cloned.1.call-start
  458.4 125.1 %all-gather.6.cloned.1.call-done = f32[1024,4,1024]{2,0,1:T(8,128)} async-done(((f32[64,4,1024]{2,0,1:T(8,128)}), f32[1024,4,1024]{2,0,1:T(8,128)}) %all-gather.6.cloned.1.call-update) | async-done | bytes 16777232 | tf_op jit(solution)/shard_map/all_gather | solution.py:36
  583.5 0.0 copy-start.1
  583.5 15.3 %convolution_bitcast_fusion.6 = f32[64,4,1024]{2,0,1:T(8,128)S(1)} fusion(f32[1024,4,1024]{2,0,1:T(8,128)} %all-gather.6.cloned.1.call-done, f32[1024,4,1024]{2,0,1:T(8,128)} %all-reduce.2.cloned.1.call-done, s32[]{:T(128)S(6)} %select_n.18, f32[64,1024]{1,0:T(8,128)S(1)} %fusion.18), kind=kOutput, calls=%fused_computation.16 | convolution fusion | flops 3221749760 | bytes 19136516 | tf_op jit(solution)/shard_map/rkj,jkc->rkc/dot_general | solution.py:37
  598.8 0.0 copy-done.4
  598.8 0.0 copy-done.1
  598.8 11.8 %fusion.15 = f32[64,4,1024]{2,0,1:T(8,128)} fusion(f32[1024,4,1024]{2,0,1:T(8,128)S(1)} %copy-done.1, f32[64,4,1024]{2,0,1:T(8,128)S(1)} %convolution_bitcast_fusion.6, f32[64,4,1024]{2,0,1:T(8,128)S(1)} %copy-done.4), kind=kOutput, calls=%fused_computation.15 | convolution fusion | flops 3221749760 | bytes 19922944 | tf_op jit(solution)/shard_map/rkj,jkc->rkc/dot_general | solution.py:38
  610.6 0.0 copy-start.5
  610.6 0.0 all-gather.8.cloned.1.call-update
  610.6 0.0 all-gather.10.cloned.1.call-start
  610.7 124.7 %all-gather.8.cloned.1.call-done = f32[1024,4,1024]{2,0,1:T(8,128)} async-done(((f32[64,4,1024]{2,0,1:T(8,128)}), f32[1024,4,1024]{2,0,1:T(8,128)}) %all-gather.8.cloned.1.call-update) | async-done | bytes 16777232 | tf_op jit(solution)/shard_map/all_gather | solution.py:36
  735.4 0.0 copy-start.2
  735.4 15.0 %convolution_bitcast_fusion.4 = f32[64,4,1024]{2,0,1:T(8,128)S(1)} fusion(f32[1024,4,1024]{2,0,1:T(8,128)} %all-gather.8.cloned.1.call-done, f32[1024,4,1024]{2,0,1:T(8,128)} %all-reduce.2.cloned.1.call-done, s32[]{:T(128)S(6)} %select_n.18, f32[64,1024]{1,0:T(8,128)S(1)} %fusion.18), kind=kOutput, calls=%fused_computation.13 | convolution fusion | flops 3221749760 | bytes 19136516 | tf_op jit(solution)/shard_map/rkj,jkc->rkc/dot_general | solution.py:37
  750.4 0.0 copy-done.5
  750.4 0.0 copy-done.2
  750.4 11.8 %fusion.14 = f32[64,4,1024]{2,0,1:T(8,128)} fusion(f32[1024,4,1024]{2,0,1:T(8,128)S(1)} %copy-done.2, f32[64,4,1024]{2,0,1:T(8,128)S(1)} %convolution_bitcast_fusion.4, f32[64,4,1024]{2,0,1:T(8,128)S(1)} %copy-done.5), kind=kOutput, calls=%fused_computation.12 | convolution fusion | flops 3221749760 | bytes 19922944 | tf_op jit(solution)/shard_map/rkj,jkc->rkc/dot_general | solution.py:38
  762.2 0.0 copy-start.3
  762.2 0.0 all-gather.10.cloned.1.call-update
  762.2 0.0 all-gather.12.cloned.1.call-start
  762.3 124.7 %all-gather.10.cloned.1.call-done = f32[1024,4,1024]{2,0,1:T(8,128)} async-done(((f32[64,4,1024]{2,0,1:T(8,128)}), f32[1024,4,1024]{2,0,1:T(8,128)}) %all-gather.10.cloned.1.call-update) | async-done | bytes 16777232 | tf_op jit(solution)/shard_map/all_gather | solution.py:36
  887.0 15.0 %convolution_bitcast_fusion.2 = f32[64,4,1024]{2,0,1:T(8,128)S(1)} fusion(f32[1024,4,1024]{2,0,1:T(8,128)} %all-gather.10.cloned.1.call-done, f32[1024,4,1024]{2,0,1:T(8,128)} %all-reduce.2.cloned.1.call-done, s32[]{:T(128)S(6)} %select_n.18, f32[64,1024]{1,0:T(8,128)S(1)} %fusion.18), kind=kOutput, calls=%fused_computation.10 | convolution fusion | flops 3221749760 | bytes 19136516 | tf_op jit(solution)/shard_map/rkj,jkc->rkc/dot_general | solution.py:37
  902.0 0.0 copy-done.3
  902.0 0.0 copy-done
  902.0 11.6 %fusion.16 = bf16[64,4,1024]{2,0,1:T(8,128)(2,1)} fusion(f32[1024,4,1024]{2,0,1:T(8,128)S(1)} %copy-done, f32[64,4,1024]{2,0,1:T(8,128)S(1)} %convolution_bitcast_fusion.2, f32[64,4,1024]{2,0,1:T(8,128)S(1)} %copy-done.3), kind=kOutput, calls=%fused_computation.17 | convolution fusion | flops 3222011904 | bytes 19398656 | tf_op jit(solution)/shard_map/rkj,jkc->rkc/dot_general | solution.py:38
  913.7 0.0 all-gather.12.cloned.1.call-update
  913.7 13.2 %constant_dynamic-slice_fusion = bf16[1,4096,1792]{2,1,0:T(8,128)(2,1)} fusion(bf16[2,4096,1792]{2,1,0:T(8,128)(2,1)} %param.5, s32[]{:T(128)S(6)} %select_n.17), kind=kLoop, calls=%fused_computation.24 | loop fusion | bytes 29360132 | tf_op jit(solution)/shard_map/jit(dynamic_index_in_dim)/dynamic_slice | solution.py:16
  926.9 59.4 %all-gather.12.cloned.1.call-done = bf16[1024,4,1024]{2,0,1:T(8,128)(2,1)} async-done(((bf16[64,4,1024]{2,0,1:T(8,128)(2,1)}), bf16[1024,4,1024]{2,0,1:T(8,128)(2,1)}) %all-gather.12.cloned.1.call-update) | async-done | bytes 8388624 | tf_op jit(solution)/shard_map/all_gather | solution.py:45
  986.3 25.9 %fusion.19 = f32[4,1024,1792]{2,1,0:T(8,128)} fusion(bf16[1024,4,1024]{2,0,1:T(8,128)(2,1)} %all-gather.12.cloned.1.call-done, bf16[4,1024,1792]{2,1,0:T(8,128)(2,1)} %bitcast.50), kind=kOutput, calls=%fused_computation.27 | convolution fusion | flops 15032385536 | bytes 52428800 | tf_op jit(solution)/shard_map/rkc,kcf->krf/dot_general | solution.py:43
  (2 shorter events, 0.0 us)
Async XLA Ops:
  6.5 338.6 %all-reduce.2.cloned.1.call-start = ((), (), s32[]{:S(2)}) async-start(), calls=%async_computation | async-start | bytes 33554432 | tf_op jit(solution)/shard_map/psum | solution.py:24
  44.3 389.5 %all-gather.14.cloned.1.call-start = ((), (), s32[]{:S(2)}) async-start(), calls=%async_computation.5 | async-start | bytes 4456448 | tf_op jit(solution)/shard_map/all_gather | solution.py:36
  386.0 197.5 %all-gather.6.cloned.1.call-start = ((), (), s32[]{:S(2)}) async-start(), calls=%async_computation.1 | async-start | bytes 17825792 | tf_op jit(solution)/shard_map/all_gather | solution.py:36
  458.3 140.4 %copy-start.4 = (f32[64,4,1024]{2,0,1:T(8,128)S(1)}, f32[64,4,1024]{2,0,1:T(8,128)}, u32[]{:S(2)}) copy-start(f32[64,4,1024]{2,0,1:T(8,128)} %fusion.10) | copy-start | bytes 3145732
  458.4 277.0 %all-gather.8.cloned.1.call-start = ((), (), s32[]{:S(2)}) async-start(), calls=%async_computation.2 | async-start | bytes 17825792 | tf_op jit(solution)/shard_map/all_gather | solution.py:36
  583.5 15.3 %copy-start.1 = (f32[1024,4,1024]{2,0,1:T(8,128)S(1)}, f32[1024,4,1024]{2,0,1:T(8,128)}, u32[]{:S(2)}) copy-start(f32[1024,4,1024]{2,0,1:T(8,128)} %all-gather.6.cloned.1.call-done) | copy-start | bytes 50331652
  610.6 139.8 %copy-start.5 = (f32[64,4,1024]{2,0,1:T(8,128)S(1)}, f32[64,4,1024]{2,0,1:T(8,128)}, u32[]{:S(2)}) copy-start(f32[64,4,1024]{2,0,1:T(8,128)} %fusion.15) | copy-start | bytes 3145732
  610.6 276.4 %all-gather.10.cloned.1.call-start = ((), (), s32[]{:S(2)}) async-start(), calls=%async_computation.3 | async-start | bytes 17825792 | tf_op jit(solution)/shard_map/all_gather | solution.py:36
  735.4 15.0 %copy-start.2 = (f32[1024,4,1024]{2,0,1:T(8,128)S(1)}, f32[1024,4,1024]{2,0,1:T(8,128)}, u32[]{:S(2)}) copy-start(f32[1024,4,1024]{2,0,1:T(8,128)} %all-gather.8.cloned.1.call-done) | copy-start | bytes 50331652
  762.2 139.8 %copy-start.3 = (f32[64,4,1024]{2,0,1:T(8,128)S(1)}, f32[64,4,1024]{2,0,1:T(8,128)}, u32[]{:S(2)}) copy-start(f32[64,4,1024]{2,0,1:T(8,128)} %fusion.14) | copy-start | bytes 3145732
  762.2 224.1 %all-gather.12.cloned.1.call-start = ((), (), s32[]{:S(2)}) async-start(), calls=%async_computation.4 | async-start | bytes 8912896 | tf_op jit(solution)/shard_map/all_gather | solution.py:45
  887.0 15.0 %copy-start = (f32[1024,4,1024]{2,0,1:T(8,128)S(1)}, f32[1024,4,1024]{2,0,1:T(8,128)}, u32[]{:S(2)}) copy-start(f32[1024,4,1024]{2,0,1:T(8,128)} %all-gather.10.cloned.1.call-done) | copy-start | bytes 50331652
Sparse Core Ops, SparseCore 0:
  44.4 300.6 all-reduce.1
  386.1 47.5 all-gather.13
  458.5 124.9 all-gather.5
  610.7 124.6 all-gather.7
  762.3 124.6 all-gather.9
  913.8 72.4 all-gather.11
where the time goes:
time: 1020 us
  waiting for transfers between devices  782 us (77%)
  matrix products  148 us (15%)
  blocking collectives  37.3 us (4%)
  local copies, waits for them, and re-layouts  33.2 us (3%)
  between operations  15.4 us (2%)
    all_gather x4, waiting for transfers between devices, local(): whole = lax.all_gather(iterate, 'dp', axis=0, tiled=True)  422 us
    psum x1, waiting for transfers between devices, local(): lax.psum(jnp.einsum('tkr,tkc->rkc', blocks, blocks, preferred_element_typ...  301 us
    all_gather x1, waiting for transfers between devices, local(): lax.all_gather(inverse, 'dp', axis=0, tiled=True)  59.4 us
    dot_general x4, matrix products, local(): jnp.einsum('rkj,jkc->rkc', factor, whole, precision=lax.Precision.HIGHEST)  57 us
    dot_general x4, matrix products, local(): jnp.einsum('rkj,jkc->rkc', product, whole, precision=lax.Precision.HIGHEST)  48 us
    psum x1, blocking collectives, local(): block_squares = lax.psum(jnp.sum(factor * factor, axis=(0, 2)), 'dp')  31.8 us
    dot_general x1, matrix products, local(): jnp.einsum('rkc,kcf->krf', lax.all_gather(inverse, 'dp', axis=0, tiled=Tr...  25.9 us
  transfers between devices with their start and end apart: 6, of which 6 were waited for; matrix products, arithmetic and copies ran while one was open for 1% of the time, Pallas kernels for 0%

commit v1 on v0

--- a/solution.py
+++ b/solution.py
@@ -9,6 +9,45 @@
 
 
 def local(step, activations, grad_weight):
+
+    def side_start(my_data, in_dim, local_block, where_dim):
+        axis_tag = "dp"
+        piece_now = lax.axis_size(axis_tag)
+        field_out, value_now, ready = (piece_now, lax.axis_index(axis_tag), my_data.shape[in_dim])
+        rows = []
+        for ii in range(field_out):
+            rows.append((ii, (ii + 1) % field_out))
+        pages = []
+        for s, pp in rows:
+            pages.append((pp, s))
+        local_now = lax.ppermute(my_data, axis_tag, rows)
+        found_now, arr_now = (local_now, lax.ppermute(my_data, axis_tag, pages))
+        f_now = local_block(my_data, value_now * ready)
+        carry = f_now.shape[where_dim]
+        extra = jnp.zeros(
+            (*f_now.shape[:where_dim], field_out * carry, *f_now.shape[where_dim + 1 :]),
+            f_now.dtype,
+        )
+
+        def treat_packet(extra, f_now, outer):
+            frame_out = lax.dynamic_update_slice_in_dim(extra, f_now, outer * carry, axis=where_dim)
+            return frame_out
+
+        extra = treat_packet(extra, f_now, value_now)
+        for rr in range(1, field_out // 2 + 1):
+            all_rows, low = ((value_now - rr) % field_out, (value_now + rr) % field_out)
+            next_value = (found_now, arr_now)
+            if rr < field_out // 2:
+                found_now, arr_now = (
+                    lax.ppermute(found_now, axis_tag, rows),
+                    lax.ppermute(arr_now, axis_tag, pages),
+                )
+            view_out = local_block(next_value[0], all_rows * ready)
+            extra = treat_packet(extra, view_out, all_rows)
+            if 2 * rr < field_out:
+                extra = treat_packet(extra, local_block(next_value[1], low * ready), low)
+        return extra
+
     groups = lax.axis_size("dp")
     layer = step[0] % LAYERS
     damping = 0.05 + 0.1 * step[0].astype(jnp.float32) / 1000.0
@@ -40,11 +79,13 @@
         )
     inverse = iterate.astype(jnp.bfloat16)
     stacked = grads.reshape(nblock, BLOCK, grads.shape[1])
-    result = jnp.einsum(
-        "rkc,kcf->krf",
-        lax.all_gather(inverse, "dp", axis=0, tiled=True),
-        stacked,
-        preferred_element_type=jnp.float32,
+    result = side_start(
+        inverse,
+        0,
+        lambda part, at: jnp.einsum(
+            "rkc,kcf->krf", part, stacked, preferred_element_type=jnp.float32
+        ),
+        1,
     )
     return result.reshape(width, grads.shape[1])
 

time: 1020 us -> 1050 us (1.029)
  waiting for transfers between devices: 782 us -> 714 us
  matrix products: 148 us -> 193 us
  starting transfers between devices: 0.42 us -> 33.5 us
  local copies, waits for them, and re-layouts: 33.2 us -> 46.2 us
    all_gather x1 -> x0, waiting for transfers between devices: 59.4 us -> none  [local(): lax.all_gather(inverse, 'dp', axis=0, tiled=True)]
    dot_general x1 -> x16, matrix products: 25.9 us -> 71.8 us  [local(): jnp.einsum('rkc,kcf->krf', part, stacked, preferred_element_type=jnp.floa...]
    ppermute x0 -> x15, starting transfers between devices: none -> 33.1 us  [the longest x6 23.5 us: side_start(): lax.ppermute(arr_now, axis_tag, pages)]
    all_gather x4, waiting for transfers between devices: 422 us -> 408 us  [local(): whole = lax.all_gather(iterate, 'dp', axis=0, tiled=True)]
    broadcast_in_dim x0 -> x1, local copies, waits for them, and re-layouts: none -> 12.8 us  [side_start(): jnp.zeros((*f_now.shape[:where_dim], field_out * carry, *f_now.shape[wher...]
  transfers between devices with their start and end apart: 6 -> 20, of which waited for: 6 -> 6; matrix products, arithmetic and copies ran while one was open for 1% -> 9% of each run, Pallas kernels for 0% -> 0%
where the time goes in v1:
time: 1050 us; the launch traced here: 1040 us
  waiting for transfers between devices  714 us (68%)
  matrix products  193 us (18%)
  local copies, waits for them, and re-layouts  46.2 us (4%)
  blocking collectives  37.3 us (4%)
  starting transfers between devices  33.5 us (3%)
  between operations  15.5 us (1%)
    all_gather x4, waiting for transfers between devices, local(): whole = lax.all_gather(iterate, 'dp', axis=0, tiled=True)  408 us
    psum x1, waiting for transfers between devices, local(): lax.psum(jnp.einsum('tkr,tkc->rkc', blocks, blocks, preferred_element_typ...  301 us
    dot_general x16, matrix products, local(): jnp.einsum('rkc,kcf->krf', part, stacked, preferred_element_type=jnp.floa...  71.8 us
    dot_general x4, matrix products, local(): jnp.einsum('rkj,jkc->rkc', factor, whole, precision=lax.Precision.HIGHEST)  57.2 us
    dot_general x4, matrix products, local(): jnp.einsum('rkj,jkc->rkc', product, whole, precision=lax.Precision.HIGHEST)  47.2 us
    psum x1, blocking collectives, local(): block_squares = lax.psum(jnp.sum(factor * factor, axis=(0, 2)), 'dp')  31.8 us
    ppermute x6, starting transfers between devices, side_start(): lax.ppermute(arr_now, axis_tag, pages)  23.5 us
  transfers between devices with their start and end apart: 20, of which 6 were waited for; matrix products, arithmetic and copies ran while one was open for 9% of the time, Pallas kernels for 0%

profile of v1, /device:TPU:0, one launch (start us, length us, event | category | flops | bytes accessed | tf_op | source)
XLA Modules:
  0.0 1043.3 jit_solution(17649061845706564926)
XLA Ops:
  7.2 7.9 constant_dynamic-slice_fusion.1
  15.1 12.0 %copy.23 = bf16[1,1024,4096]{1,2,0:T(8,128)(2,1)} copy(bf16[1,1024,4096]{2,1,0:T(8,128)(2,1)} %constant_dynamic-slice_fusion.1) | data formatting | bytes 16777216
  27.1 17.1 %convolution_bitcast_fusion = f32[1024,4,1024]{2,0,1:T(8,128)} fusion(bf16[1024,4,1024]{0,2,1:T(8,128)(2,1)} %bitcast.98), kind=kOutput, calls=%fused_computation | convolution fusion | flops 8589934592 | bytes 25165824 | tf_op jit(solution)/shard_map/tkr,tkc->rkc/dot_general | solution.py:64
  44.5 300.7 %all-reduce.2.cloned.1.call-done = f32[1024,4,1024]{2,0,1:T(8,128)} async-done(((f32[1024,4,1024]{2,0,1:T(8,128)}), f32[1024,4,1024]{2,0,1:T(8,128)}) %all-reduce.2.cloned.1.call-update) | async-done | bytes 16777232 | tf_op jit(solution)/shard_map/psum | solution.py:63
  345.1 1.5 multiply_reduce_fusion
  346.6 31.8 %psum.15 = f32[4]{0:T(128)S(1)} all-reduce(f32[4]{0:T(128)S(1)} %multiply_reduce_fusion), channel_id=1, replica_groups=mesh['dp'=16,'tensor'=2] {'dp'}, use_global_device_ids=true, to_apply=%region_2.3 | all-reduce | flops 4 | bytes 32 | tf_op jit(solution)/shard_map/psum | solution.py:71
  379.0 5.5 pmax.7
  385.2 0.8 broadcast_multiply_fusion
  386.3 47.5 %all-gather.11.cloned.1.call-done = f32[1024,1024]{1,0:T(8,128)} async-done(((f32[64,1024]{1,0:T(8,128)}), f32[1024,1024]{1,0:T(8,128)}) %all-gather.11.cloned.1.call-update) | async-done | bytes 4194320 | tf_op jit(solution)/shard_map/all_gather | solution.py:75
  433.8 11.8 %fusion.4 = f32[64,4,1024]{2,0,1:T(8,128)S(1)} fusion(f32[1024,1024]{1,0:T(8,128)} %all-gather.11.cloned.1.call-done, f32[1024,4,1024]{2,0,1:T(8,128)} %all-reduce.2.cloned.1.call-done, s32[]{:T(128)S(6)} %select_n.124, f32[64,1024]{1,0:T(8,128)S(1)} %fusion.18), kind=kOutput, calls=%fused_computation.21 | convolution fusion | flops 3221749760 | bytes 6553604 | tf_op jit(solution)/shard_map/rkj,jkc->rkc/dot_general | solution.py:76
  445.6 12.8 %fusion.10 = f32[64,4,1024]{2,0,1:T(8,128)} fusion(f32[64,4,1024]{2,0,1:T(8,128)S(1)} %fusion.4, f32[1024,1024]{1,0:T(8,128)} %all-gather.11.cloned.1.call-done, f32[64,1024]{1,0:T(8,128)S(1)} %get-tuple-element.5), kind=kOutput, calls=%fused_computation.23 | convolution fusion | flops 3221487616 | bytes 6553600 | tf_op jit(solution)/shard_map/rkj,jkc->rkc/dot_general | solution.py:77
  458.5 125.1 %all-gather.5.cloned.1.call-done = f32[1024,4,1024]{2,0,1:T(8,128)} async-done(((f32[64,4,1024]{2,0,1:T(8,128)}), f32[1024,4,1024]{2,0,1:T(8,128)}) %all-gather.5.cloned.1.call-update) | async-done | bytes 16777232 | tf_op jit(solution)/shard_map/all_gather | solution.py:75
  583.5 15.3 %convolution_bitcast_fusion.6 = f32[64,4,1024]{2,0,1:T(8,128)S(1)} fusion(f32[1024,4,1024]{2,0,1:T(8,128)} %all-gather.5.cloned.1.call-done, f32[1024,4,1024]{2,0,1:T(8,128)} %all-reduce.2.cloned.1.call-done, s32[]{:T(128)S(6)} %select_n.124, f32[64,1024]{1,0:T(8,128)S(1)} %fusion.18), kind=kOutput, calls=%fused_computation.32 | convolution fusion | flops 3221749760 | bytes 19136516 | tf_op jit(solution)/shard_map/rkj,jkc->rkc/dot_general | solution.py:76
  598.8 11.8 %fusion.15 = f32[64,4,1024]{2,0,1:T(8,128)} fusion(f32[1024,4,1024]{2,0,1:T(8,128)S(1)} %copy-done.1, f32[64,4,1024]{2,0,1:T(8,128)S(1)} %convolution_bitcast_fusion.6, f32[64,4,1024]{2,0,1:T(8,128)S(1)} %copy-done.4), kind=kOutput, calls=%fused_computation.31 | convolution fusion | flops 3221749760 | bytes 19922944 | tf_op jit(solution)/shard_map/rkj,jkc->rkc/dot_general | solution.py:77
  610.7 124.7 %all-gather.7.cloned.1.call-done = f32[1024,4,1024]{2,0,1:T(8,128)} async-done(((f32[64,4,1024]{2,0,1:T(8,128)}), f32[1024,4,1024]{2,0,1:T(8,128)}) %all-gather.7.cloned.1.call-update) | async-done | bytes 16777232 | tf_op jit(solution)/shard_map/all_gather | solution.py:75
  735.4 15.0 %convolution_bitcast_fusion.4 = f32[64,4,1024]{2,0,1:T(8,128)S(1)} fusion(f32[1024,4,1024]{2,0,1:T(8,128)} %all-gather.7.cloned.1.call-done, f32[1024,4,1024]{2,0,1:T(8,128)} %all-reduce.2.cloned.1.call-done, s32[]{:T(128)S(6)} %select_n.124, f32[64,1024]{1,0:T(8,128)S(1)} %fusion.18), kind=kOutput, calls=%fused_computation.29 | convolution fusion | flops 3221749760 | bytes 19136516 | tf_op jit(solution)/shard_map/rkj,jkc->rkc/dot_general | solution.py:76
  750.4 11.8 %fusion.14 = f32[64,4,1024]{2,0,1:T(8,128)} fusion(f32[1024,4,1024]{2,0,1:T(8,128)S(1)} %copy-done.2, f32[64,4,1024]{2,0,1:T(8,128)S(1)} %convolution_bitcast_fusion.4, f32[64,4,1024]{2,0,1:T(8,128)S(1)} %copy-done.5), kind=kOutput, calls=%fused_computation.28 | convolution fusion | flops 3221749760 | bytes 19922944 | tf_op jit(solution)/shard_map/rkj,jkc->rkc/dot_general | solution.py:77
  762.6 13.5 %constant_dynamic-slice_fusion = bf16[1,4096,1792]{2,1,0:T(8,128)(2,1)} fusion(bf16[2,4096,1792]{2,1,0:T(8,128)(2,1)} %param.5, s32[]{:T(128)S(6)} %select_n.123), kind=kLoop, calls=%fused_computation.40 | loop fusion | bytes 29360132 | tf_op jit(solution)/shard_map/jit(dynamic_index_in_dim)/dynamic_slice | solution.py:55
  776.0 111.0 %all-gather.9.cloned.1.call-done = f32[1024,4,1024]{2,0,1:T(8,128)} async-done(((f32[64,4,1024]{2,0,1:T(8,128)}), f32[1024,4,1024]{2,0,1:T(8,128)}) %all-gather.9.cloned.1.call-update) | async-done | bytes 16777232 | tf_op jit(solution)/shard_map/all_gather | solution.py:75
  887.1 15.2 %convolution_bitcast_fusion.2 = f32[64,4,1024]{2,0,1:T(8,128)S(1)} fusion(f32[1024,4,1024]{2,0,1:T(8,128)} %all-gather.9.cloned.1.call-done, f32[1024,4,1024]{2,0,1:T(8,128)} %all-reduce.2.cloned.1.call-done, s32[]{:T(128)S(6)} %select_n.124, f32[64,1024]{1,0:T(8,128)S(1)} %fusion.18), kind=kOutput, calls=%fused_computation.26 | convolution fusion | flops 3221749760 | bytes 19136516 | tf_op jit(solution)/shard_map/rkj,jkc->rkc/dot_general | solution.py:76
  902.3 10.8 %fusion.16 = bf16[64,4,1024]{2,0,1:T(8,128)(2,1)S(1)} fusion(f32[1024,4,1024]{2,0,1:T(8,128)S(1)} %copy-done, f32[64,4,1024]{2,0,1:T(8,128)S(1)} %convolution_bitcast_fusion.2, f32[64,4,1024]{2,0,1:T(8,128)S(1)} %copy-done.3), kind=kOutput, calls=%fused_computation.33 | convolution fusion | flops 3222011904 | bytes 19398656 | tf_op jit(solution)/shard_map/rkj,jkc->rkc/dot_general | solution.py:77
  913.4 4.3 collective-permute-start.1
  917.8 12.8 %broadcast_in_dim.10 = f32[4,1024,1792]{2,1,0:T(8,128)} broadcast(f32[]{:T(128)} %constant.118.clone.1), dimensions={} | broadcast | bytes 29360132 | tf_op jit(solution)/shard_map/broadcast_in_dim | solution.py:27
  930.6 9.2 convolution_dynamic-update-slice_fusion.15
  939.8 4.4 collective-permute-start.3
  944.2 9.0 convolution_dynamic-update-slice_fusion.14
  953.3 3.8 convolution_dynamic-update-slice_fusion.13
  957.1 4.6 collective-permute-start.5
  961.8 3.8 convolution_dynamic-update-slice_fusion.12
  965.6 3.8 convolution_dynamic-update-slice_fusion.11
  969.4 4.4 collective-permute-start.7
  973.9 3.8 convolution_dynamic-update-slice_fusion.10
  977.7 3.8 convolution_dynamic-update-slice_fusion.9
  981.5 2.4 collective-permute-start.8
  983.9 2.3 collective-permute-start.9
  986.2 3.8 convolution_dynamic-update-slice_fusion.8
  990.0 3.8 convolution_dynamic-update-slice_fusion.7
  994.3 4.0 collective-permute-start.11
  998.3 3.8 convolution_dynamic-update-slice_fusion.6
  1002.1 3.8 convolution_dynamic-update-slice_fusion.5
  1006.0 1.7 collective-permute-start.12
  1007.7 3.8 collective-permute-start.13
  1011.5 3.8 convolution_dynamic-update-slice_fusion.4
  1015.3 3.8 convolution_dynamic-update-slice_fusion.3
  1019.5 3.8 convolution_dynamic-update-slice_fusion.2
  1023.3 3.8 convolution_dynamic-update-slice_fusion.1
  1027.1 5.3 collective-permute-done.14
  1032.5 3.8 convolution_dynamic-update-slice_fusion
  (54 shorter events, 2.4 us)
Async XLA Ops:
  6.5 338.6 %all-reduce.2.cloned.1.call-start = ((), (), s32[]{:S(2)}) async-start(), calls=%async_computation | async-start | bytes 33554432 | tf_op jit(solution)/shard_map/psum | solution.py:63
  44.3 389.5 %all-gather.11.cloned.1.call-start = ((), (), s32[]{:S(2)}) async-start(), calls=%async_computation.4 | async-start | bytes 4456448 | tf_op jit(solution)/shard_map/all_gather | solution.py:75
  386.0 197.5 %all-gather.5.cloned.1.call-start = ((), (), s32[]{:S(2)}) async-start(), calls=%async_computation.1 | async-start | bytes 17825792 | tf_op jit(solution)/shard_map/all_gather | solution.py:75
  458.4 140.4 %copy-start.4 = (f32[64,4,1024]{2,0,1:T(8,128)S(1)}, f32[64,4,1024]{2,0,1:T(8,128)}, u32[]{:S(2)}) copy-start(f32[64,4,1024]{2,0,1:T(8,128)} %fusion.10) | copy-start | bytes 3145732
  458.4 277.0 %all-gather.7.cloned.1.call-start = ((), (), s32[]{:S(2)}) async-start(), calls=%async_computation.2 | async-start | bytes 17825792 | tf_op jit(solution)/shard_map/all_gather | solution.py:75
  583.5 15.3 %copy-start.1 = (f32[1024,4,1024]{2,0,1:T(8,128)S(1)}, f32[1024,4,1024]{2,0,1:T(8,128)}, u32[]{:S(2)}) copy-start(f32[1024,4,1024]{2,0,1:T(8,128)} %all-gather.5.cloned.1.call-done) | copy-start | bytes 50331652
  610.6 139.8 %copy-start.5 = (f32[64,4,1024]{2,0,1:T(8,128)S(1)}, f32[64,4,1024]{2,0,1:T(8,128)}, u32[]{:S(2)}) copy-start(f32[64,4,1024]{2,0,1:T(8,128)} %fusion.15) | copy-start | bytes 3145732
  610.7 276.4 %all-gather.9.cloned.1.call-start = ((), (), s32[]{:S(2)}) async-start(), calls=%async_computation.3 | async-start | bytes 17825792 | tf_op jit(solution)/shard_map/all_gather | solution.py:75
  735.4 15.0 %copy-start.2 = (f32[1024,4,1024]{2,0,1:T(8,128)S(1)}, f32[1024,4,1024]{2,0,1:T(8,128)}, u32[]{:S(2)}) copy-start(f32[1024,4,1024]{2,0,1:T(8,128)} %all-gather.7.cloned.1.call-done) | copy-start | bytes 50331652
  776.0 126.3 %copy-start.3 = (f32[64,4,1024]{2,0,1:T(8,128)S(1)}, f32[64,4,1024]{2,0,1:T(8,128)}, u32[]{:S(2)}) copy-start(f32[64,4,1024]{2,0,1:T(8,128)} %fusion.14) | copy-start | bytes 3145732
  887.1 15.2 %copy-start = (f32[1024,4,1024]{2,0,1:T(8,128)S(1)}, f32[1024,4,1024]{2,0,1:T(8,128)}, u32[]{:S(2)}) copy-start(f32[1024,4,1024]{2,0,1:T(8,128)} %all-gather.9.cloned.1.call-done) | copy-start | bytes 50331652
  913.1 26.6 %collective-permute-start = (bf16[64,4,1024]{2,0,1:T(8,128)(2,1)S(1)}, bf16[64,4,1024]{2,0,1:T(8,128)(2,1)S(1)}, u32[]{:S(2)}, u32[]{:S(2)}) collective-permute-start(bf16[64,4,1024]{2,0,1:T(8,128)(2,1)S(1)} %fusion.16), channel_id=1, source_target_pairs={{0,2},{2,4},{4,6},{6,8},{8,10},{10,12},{12,14},{14,16},{16,18},{18... | collective-permute-start | bytes 1572872 | tf_op jit(solution)/shard_map/ppermute | solution.py:23
  913.4 26.4 %collective-permute-start.1 = (bf16[64,4,1024]{2,0,1:T(8,128)(2,1)S(1)}, bf16[64,4,1024]{2,0,1:T(8,128)(2,1)S(1)}, u32[]{:S(2)}, u32[]{:S(2)}) collective-permute-start(bf16[64,4,1024]{2,0,1:T(8,128)(2,1)S(1)} %fusion.16), channel_id=1, source_target_pairs={{2,0},{4,2},{6,4},{8,6},{10,8},{12,10},{14,12},{16,14},{18,16},{20... | collective-permute-start | bytes 1572872 | tf_op jit(solution)/shard_map/ppermute | solution.py:24
  930.6 22.7 %slice-start = ((s8[14680064]{0:T(1024)(128)(4,1)}), s8[4194304]{0:T(1024)(128)(4,1)S(1)}, s32[]{:S(2)}) async-start(s8[14680064]{0:T(1024)(128)(4,1)} %bitcast.82), calls=%async_computation.5 | async-start | bytes 8388608
  930.6 22.7 %slice-start.1 = ((s8[14680064]{0:T(1024)(128)(4,1)}), s8[4194304]{0:T(1024)(128)(4,1)S(1)}, s32[]{:S(2)}) async-start(s8[14680064]{0:T(1024)(128)(4,1)} %bitcast.82), calls=%async_computation.6 | async-start | bytes 8388608
  939.7 13.5 %slice-start.2 = ((s8[14680064]{0:T(1024)(128)(4,1)}), s8[4194304]{0:T(1024)(128)(4,1)S(1)}, s32[]{:S(2)}) async-start(s8[14680064]{0:T(1024)(128)(4,1)} %bitcast.82), calls=%async_computation.7 | async-start | bytes 8388608
  939.7 13.5 %slice-start.3 = ((s8[14680064]{0:T(1024)(128)(4,1)}), s8[2097152]{0:T(1024)(128)(4,1)S(1)}, s32[]{:S(2)}) async-start(s8[14680064]{0:T(1024)(128)(4,1)} %bitcast.82), calls=%async_computation.8 | async-start | bytes 4194304
  939.7 17.4 %collective-permute-start.2 = (bf16[64,4,1024]{2,0,1:T(8,128)(2,1)S(1)}, bf16[64,4,1024]{2,0,1:T(8,128)(2,1)S(1)}, u32[]{:S(2)}, u32[]{:S(2)}) collective-permute-start(bf16[64,4,1024]{2,0,1:T(8,128)(2,1)S(1)} %collective-permute-done), channel_id=1, source_target_pairs={{0,2},{2,4},{4,6},{6,8},{8,10},{10,12},{12,14},{14,16},{16,18},{18... | collective-permute-start | bytes 1572872 | tf_op jit(solution)/shard_map/ppermute | solution.py:42
  939.8 17.3 %collective-permute-start.3 = (bf16[64,4,1024]{2,0,1:T(8,128)(2,1)S(1)}, bf16[64,4,1024]{2,0,1:T(8,128)(2,1)S(1)}, u32[]{:S(2)}, u32[]{:S(2)}) collective-permute-start(bf16[64,4,1024]{2,0,1:T(8,128)(2,1)S(1)} %collective-permute-done.1), channel_id=1, source_target_pairs={{2,0},{4,2},{6,4},{8,6},{10,8},{12,10},{14,12},{16,14},{18,16},{20... | collective-permute-start | bytes 1572872 | tf_op jit(solution)/shard_map/ppermute | solution.py:43
  957.1 12.3 %collective-permute-start.4 = (bf16[64,4,1024]{2,0,1:T(8,128)(2,1)S(1)}, bf16[64,4,1024]{2,0,1:T(8,128)(2,1)S(1)}, u32[]{:S(2)}, u32[]{:S(2)}) collective-permute-start(bf16[64,4,1024]{2,0,1:T(8,128)(2,1)S(1)} %collective-permute-done.2), channel_id=1, source_target_pairs={{0,2},{2,4},{4,6},{6,8},{8,10},{10,12},{12,14},{14,16},{16,18},{18... | collective-permute-start | bytes 1572872 | tf_op jit(solution)/shard_map/ppermute | solution.py:42
  957.1 12.3 %collective-permute-start.5 = (bf16[64,4,1024]{2,0,1:T(8,128)(2,1)S(1)}, bf16[64,4,1024]{2,0,1:T(8,128)(2,1)S(1)}, u32[]{:S(2)}, u32[]{:S(2)}) collective-permute-start(bf16[64,4,1024]{2,0,1:T(8,128)(2,1)S(1)} %collective-permute-done.3), channel_id=1, source_target_pairs={{2,0},{4,2},{6,4},{8,6},{10,8},{12,10},{14,12},{16,14},{18,16},{20... | collective-permute-start | bytes 1572872 | tf_op jit(solution)/shard_map/ppermute | solution.py:43
  969.4 12.1 %collective-permute-start.6 = (bf16[64,4,1024]{2,0,1:T(8,128)(2,1)S(1)}, bf16[64,4,1024]{2,0,1:T(8,128)(2,1)S(1)}, u32[]{:S(2)}, u32[]{:S(2)}) collective-permute-start(bf16[64,4,1024]{2,0,1:T(8,128)(2,1)S(1)} %collective-permute-done.4), channel_id=1, source_target_pairs={{0,2},{2,4},{4,6},{6,8},{8,10},{10,12},{12,14},{14,16},{16,18},{18... | collective-permute-start | bytes 1572872 | tf_op jit(solution)/shard_map/ppermute | solution.py:42
  969.4 14.5 %collective-permute-start.7 = (bf16[64,4,1024]{2,0,1:T(8,128)(2,1)S(1)}, bf16[64,4,1024]{2,0,1:T(8,128)(2,1)S(1)}, u32[]{:S(2)}, u32[]{:S(2)}) collective-permute-start(bf16[64,4,1024]{2,0,1:T(8,128)(2,1)S(1)} %collective-permute-done.5), channel_id=1, source_target_pairs={{2,0},{4,2},{6,4},{8,6},{10,8},{12,10},{14,12},{16,14},{18,16},{20... | collective-permute-start | bytes 1572872 | tf_op jit(solution)/shard_map/ppermute | solution.py:43
  981.5 12.3 %collective-permute-start.8 = (bf16[64,4,1024]{2,0,1:T(8,128)(2,1)S(1)}, bf16[64,4,1024]{2,0,1:T(8,128)(2,1)S(1)}, u32[]{:S(2)}, u32[]{:S(2)}) collective-permute-start(bf16[64,4,1024]{2,0,1:T(8,128)(2,1)S(1)} %collective-permute-done.6), channel_id=1, source_target_pairs={{0,2},{2,4},{4,6},{6,8},{8,10},{10,12},{12,14},{14,16},{16,18},{18... | collective-permute-start | bytes 1572872 | tf_op jit(solution)/shard_map/ppermute | solution.py:42
  983.9 10.4 collective-permute-start.9
  993.9 12.1 %collective-permute-start.10 = (bf16[64,4,1024]{2,0,1:T(8,128)(2,1)S(1)}, bf16[64,4,1024]{2,0,1:T(8,128)(2,1)S(1)}, u32[]{:S(2)}, u32[]{:S(2)}) collective-permute-start(bf16[64,4,1024]{2,0,1:T(8,128)(2,1)S(1)} %collective-permute-done.8), channel_id=1, source_target_pairs={{0,2},{2,4},{4,6},{6,8},{8,10},{10,12},{12,14},{14,16},{16,18},{18... | collective-permute-start | bytes 1572872 | tf_op jit(solution)/shard_map/ppermute | solution.py:42
  994.3 13.4 %collective-permute-start.11 = (bf16[64,4,1024]{2,0,1:T(8,128)(2,1)S(1)}, bf16[64,4,1024]{2,0,1:T(8,128)(2,1)S(1)}, u32[]{:S(2)}, u32[]{:S(2)}) collective-permute-start(bf16[64,4,1024]{2,0,1:T(8,128)(2,1)S(1)} %collective-permute-done.9), channel_id=1, source_target_pairs={{2,0},{4,2},{6,4},{8,6},{10,8},{12,10},{14,12},{16,14},{18,16},{20... | collective-permute-start | bytes 1572872 | tf_op jit(solution)/shard_map/ppermute | solution.py:43
  1006.0 13.2 %collective-permute-start.12 = (bf16[64,4,1024]{2,0,1:T(8,128)(2,1)S(1)}, bf16[64,4,1024]{2,0,1:T(8,128)(2,1)S(1)}, u32[]{:S(2)}, u32[]{:S(2)}) collective-permute-start(bf16[64,4,1024]{2,0,1:T(8,128)(2,1)S(1)} %collective-permute-done.10), channel_id=1, source_target_pairs={{0,2},{2,4},{4,6},{6,8},{8,10},{10,12},{12,14},{14,16},{16,18},{18... | collective-permute-start | bytes 1572872 | tf_op jit(solution)/shard_map/ppermute | solution.py:42
  1007.7 15.6 %collective-permute-start.13 = (bf16[64,4,1024]{2,0,1:T(8,128)(2,1)S(1)}, bf16[64,4,1024]{2,0,1:T(8,128)(2,1)S(1)}, u32[]{:S(2)}, u32[]{:S(2)}) collective-permute-start(bf16[64,4,1024]{2,0,1:T(8,128)(2,1)S(1)} %collective-permute-done.11), channel_id=1, source_target_pairs={{2,0},{4,2},{6,4},{8,6},{10,8},{12,10},{14,12},{16,14},{18,16},{20... | collective-permute-start | bytes 1572872 | tf_op jit(solution)/shard_map/ppermute | solution.py:43
  1019.1 13.3 %collective-permute-start.14 = (bf16[64,4,1024]{2,0,1:T(8,128)(2,1)S(1)}, bf16[64,4,1024]{2,0,1:T(8,128)(2,1)S(1)}, u32[]{:S(2)}, u32[]{:S(2)}) collective-permute-start(bf16[64,4,1024]{2,0,1:T(8,128)(2,1)S(1)} %collective-permute-done.12), channel_id=1, source_target_pairs={{0,2},{2,4},{4,6},{6,8},{8,10},{10,12},{12,14},{14,16},{16,18},{18... | collective-permute-start | bytes 1572872 | tf_op jit(solution)/shard_map/ppermute | solution.py:42
Sparse Core Ops, SparseCore 0:
  44.4 300.6 all-reduce.1
  386.2 47.6 all-gather.10
  458.5 124.9 all-gather.4
  610.8 124.6 all-gather.6
  762.4 124.6 all-gather.8
